TPU v7x, 256 devices: a whole 4x4x8 slice. The times are simulated.
256 devices in a mesh: sta: 16 (over y, x), evt: 16 (over z, core).
Axes of the slice: x: 4, y: 4, z: 8, core: 2. Of those that a mesh axis runs over, the one named last changes fastest.
Arguments:
- traces: bfloat16 [3, 128, 1024, 2048], P(None, 'sta', 'evt'), may hold values from -96 to 96
- baz_bin: int32 [128, 1024], P('sta', 'evt'), may hold values from 0 to 35
- inc_bin: int32 [128, 1024], P('sta', 'evt'), may hold values from 0 to 7
- counts: int32 [128], P('sta'), may hold values from 128 to 1024
- depth_index: int32 [128, 512], P('sta'), may hold values from 0 to 2046
- tile_of: int32 [128], replicated, may hold values from 0 to 63
Outputs:
- stack: float32 [64, 5, 2, 512], P('sta', None, None, 'evt')
All inputs are finite; a program needn't handle non-finite values.
Results may differ from a plain program's by a relative error of at most 0.0003.
Values sent between devices are 32-bit elements; how exact they have to be, the bound alone decides.
No kernel may reach another device: no remote copies, remote signals or barrier semaphores. Data moves between devices by JAX's collectives and lax.ppermute only.
A program may use at most 64 MiB of HBM per device.

v0:
```python
import jax
import jax.numpy as jnp
from jax import lax
from jax.sharding import PartitionSpec as P

NS = 2048
DEPTHS = 512
BAZ_BINS = 36
TILE_DEV = 4


def from_everyone(value, axis):
    size = lax.axis_size(axis)
    return lax.all_to_all(
        jnp.broadcast_to(value[None], (size, *value.shape)), axis, 0, 0, tiled=True
    )


def over_copies(value, axis):
    return from_everyone(value, axis).sum(axis=0)


def in_blocks(value, dim, size):
    shape = value.shape
    parts = value.reshape(*shape[:dim], size, shape[dim] // size, *shape[dim + 1 :])
    return jnp.moveaxis(parts, dim, 0)


def summed_on_arrival(value, axis, dim):
    parts = in_blocks(value, dim, lax.axis_size(axis))
    arrived = lax.all_to_all(parts, axis, split_axis=0, concat_axis=0, tiled=True)
    return arrived.sum(axis=0)


def joined_along(parts, dim):
    parts = jnp.moveaxis(parts, 0, dim)
    shape = parts.shape
    return parts.reshape(*shape[:dim], shape[dim] * shape[dim + 1], *shape[dim + 2 :])


def gather_directly(value, axis, dim):
    parts = from_everyone(value, axis)
    return joined_along(parts, dim)


def solve_blocks(normal, right):
    factor = jnp.linalg.cholesky(normal)
    middle = jax.scipy.linalg.solve_triangular(factor, right, lower=True)
    return jax.scipy.linalg.solve_triangular(factor, middle, lower=True, trans=1)


def to_depths(values, indices):
    picks = indices[:, None, None, :]
    first = jnp.take_along_axis(values, picks, axis=3)
    second = jnp.take_along_axis(values, picks + 1, axis=3)
    return 0.5 * (first + second)


def body(traces, baz_bin, inc_bin, counts, depth_index, tile_of):
    highest = lax.Precision.HIGHEST
    stations = traces.shape[1]
    slots = traces.shape[2]
    evt_count = lax.axis_size("evt")
    depth_share = DEPTHS // evt_count
    phi = (baz_bin.astype(jnp.float32) + 0.5) * (2.0 * jnp.pi / BAZ_BINS)
    incidence = (12.0 + 2.5 * (inc_bin.astype(jnp.float32) + 0.5)) * (jnp.pi / 180.0)
    cosine = jnp.cos(phi)[:, :, None]
    sine = jnp.sin(phi)[:, :, None]
    vertical = traces[0].astype(jnp.float32)
    north = traces[1].astype(jnp.float32)
    east = traces[2].astype(jnp.float32)
    radial = -(cosine * north + sine * east)
    quality = jnp.cos(incidence)[:, :, None] * radial + jnp.sin(incidence)[:, :, None] * vertical
    transverse = sine * north - cosine * east
    data = jnp.concatenate([quality, transverse], axis=2)
    slot_ids = lax.axis_index("evt") * slots + jnp.arange(slots)
    live = (slot_ids[None, :] < counts[:, None]).astype(jnp.float32)
    harm = jnp.stack(
        [jnp.ones_like(phi), jnp.cos(phi), jnp.sin(phi), jnp.cos(2.0 * phi), jnp.sin(2.0 * phi)],
        axis=2,
    )
    weighted = harm * live[:, :, None]
    normal_part = jnp.einsum("sek,sel->skl", weighted, harm, precision=highest)
    rhs_part = jnp.einsum("sek,sec->skc", weighted, data, precision=highest)
    normal = over_copies(normal_part, "evt") + jnp.eye(5, dtype=jnp.float32)[None]
    shares = summed_on_arrival(rhs_part, "evt", 2)
    solved = solve_blocks(normal, shares)
    coeff = gather_directly(solved, "evt", 2).reshape(stations, 5, 2, NS)
    mine = lax.dynamic_slice_in_dim(
        depth_index, lax.axis_index("evt") * depth_share, depth_share, 1
    )
    profile = to_depths(coeff, mine)
    first_tile = lax.axis_index("sta") * TILE_DEV
    own_tiles = first_tile + jnp.arange(TILE_DEV)
    members = jnp.sum((tile_of[None, :] == own_tiles[:, None]).astype(jnp.float32), axis=1)
    tile_total = TILE_DEV * lax.axis_size("sta")
    local_tiles = lax.dynamic_slice_in_dim(tile_of, lax.axis_index("sta") * stations, stations, 0)
    onehot = (local_tiles[None, :] == jnp.arange(tile_total)[:, None]).astype(jnp.float32)
    partial_sums = jnp.einsum("ts,skcz->tkcz", onehot, profile, precision=highest)
    sums = summed_on_arrival(partial_sums, "sta", 0)
    return sums / jnp.maximum(members, 1.0)[:, None, None, None]


def solution(mesh):
    return jax.shard_map(
        body,
        mesh=mesh,
        in_specs=(
            P(None, "sta", "evt", None),
            P("sta", "evt"),
            P("sta", "evt"),
            P("sta"),
            P("sta", None),
            P(),
        ),
        out_specs=P("sta", None, None, "evt"),
        check_vma=False,
    )
```

profile of v0, /device:TPU:1, one launch (start us, length us, event | category | flops | bytes accessed | tf_op | source)
XLA Modules:
  0.0 122.7 jit_solution(14298192533646894281)
XLA Ops:
  0.0 0.8 fusion.38
  0.8 0.7 compare_convert_fusion
  1.5 0.2 fusion.12
  1.8 0.8 reshape.141
  2.6 10.0 %all-to-all-start = ((f32[16,1,200]{2,1,0:T(1,128)}), f32[16,1,200]{2,1,0:T(1,128)S(1)}, u32[]{:S(2)}, u32[]{:S(2)}) async-start(f32[16,1,200]{2,1,0:T(1,128)} %reshape.141), calls=%async_computation | async-start | bytes 32768 | tf_op jit(solution)/shard_map/all_to_all | solution.py:14
  12.6 4.3 %fusion.7 = (f32[8,64,2048]{2,1,0:T(8,128)S(1)}, f32[8,64,2048]{2,1,0:T(8,128)S(1)}) fusion(bf16[3,8,64,2048]{3,2,1,0:T(8,128)(2,1)} %param.8, f32[8,64]{1,0:T(8,128)S(1)} %get-tuple-element.18, f32[8,64]{1,0:T(8,128)S(1)} %get-tuple-element.13, f32[8,64]{1,0:T(8,128)S(1)} %get-tuple-element.15, f32[8,64]{1,0:T(8,128)S(1)} %get-tuple-element.19), kind=kLoop, calls=%fused_computation.13 | loop fusion | flops 13631488 | bytes 14688256 | tf_op jit(solution)/shard_map/add | solution.py:73
  16.9 4.0 %fusion = f32[8,5,4096]{2,1,0:T(8,128)S(1)} fusion(f32[8,64,2048]{2,1,0:T(8,128)S(1)} %get-tuple-element.7, f32[8,64,2048]{2,1,0:T(8,128)S(1)} %get-tuple-element.6, f32[8,64,5]{1,2,0:T(8,128)S(1)} %stack.19, f32[8,64]{1,0:T(8,128)S(1)} %compare_convert_fusion), kind=kOutput, calls=%fused_computation.2 | convolution fusion | flops 127928832 | bytes 9056256 | tf_op jit(solution)/shard_map/sek,sec->skc/dot_general | solution.py:84
  21.0 0.3 reshape.140
  21.3 1.2 copy.71
  22.6 7.2 %all-to-all-start.1 = ((f32[16,8,5,256]{3,1,2,0:T(8,128)}), f32[16,8,5,256]{3,1,2,0:T(8,128)S(1)}, u32[]{:S(2)}, u32[]{:S(2)}) async-start(f32[16,8,5,256]{3,1,2,0:T(8,128)} %copy.71), calls=%async_computation.1 | async-start | bytes 1310720 | tf_op jit(solution)/shard_map/all_to_all | solution.py:31
  29.8 0.5 broadcast.219
  30.3 0.7 reduce.6
  31.4 3.7 %custom-call.11 = f32[8,5,5]{2,1,0:T(8,128)S(1)} custom-call(f32[8,5,5]{2,1,0:T(8,128)S(1)} %fusion.24), custom_call_target="Cholesky" | custom-call | tf_op jit(solution)/shard_map/jit(cholesky)/cholesky | solution.py:47
  35.3 3.2 %custom-call.12 = f32[8,1,5,5]{2,3,1,0:T(8,128)S(1)} custom-call(f32[8,1,5,5]{3,2,1,0:T(8,128)S(1)} %select_bitcast_fusion), custom_call_target="InvertDiagBlocksLowerTriangular" | custom-call | tf_op jit(solution)/shard_map/jit(_solve_triangular)/vmap()/triangular_solve | solution.py:49
  38.5 11.2 %all-to-all-done.1 = f32[16,8,5,256]{3,1,2,0:T(8,128)S(1)} async-done(((f32[16,8,5,256]{3,1,2,0:T(8,128)}), f32[16,8,5,256]{3,1,2,0:T(8,128)S(1)}, u32[]{:S(2)}, u32[]{:S(2)}) %all-to-all-start.1) | async-done | bytes 655392 | tf_op jit(solution)/shard_map/all_to_all | solution.py:31
  49.8 0.3 fusion.9
  50.0 0.2 fusion.20
  50.2 0.9 broadcast_in_dim.13
  51.1 3.5 %all-to-all-start.2 = ((f32[16,8,5,256]{3,1,2,0:T(8,128)}), f32[16,8,5,256]{3,1,2,0:T(8,128)S(1)}, u32[]{:S(2)}, u32[]{:S(2)}) async-start(f32[16,8,5,256]{3,1,2,0:T(8,128)} %broadcast_in_dim.13), calls=%async_computation.2 | async-start | bytes 1310720 | tf_op jit(solution)/shard_map/all_to_all | solution.py:14
  55.2 19.0 %all-to-all-done.2 = f32[16,8,5,256]{3,1,2,0:T(8,128)S(1)} async-done(((f32[16,8,5,256]{3,1,2,0:T(8,128)}), f32[16,8,5,256]{3,1,2,0:T(8,128)S(1)}, u32[]{:S(2)}, u32[]{:S(2)}) %all-to-all-start.2) | async-done | bytes 655392 | tf_op jit(solution)/shard_map/all_to_all | solution.py:14
  74.2 0.2 copy.76
  74.4 0.4 reshape_reshape.3
  74.8 17.0 %copy.77 = f32[8,5,2,2048]{1,2,3,0:T(2,128)} copy(f32[8,5,2,2048]{3,2,1,0:T(2,128)S(1)} %reshape_reshape.3) | data formatting | bytes 1310720 | tf_op jit(solution)/shard_map/reshape;reshape | solution.py:88
  91.8 7.0 %gather_fusion = f32[256,5,2]{1,2,0:T(2,128)S(1)} fusion(f32[8,5,2,2048]{1,2,3,0:T(2,128)} %copy.77, s32[256]{0:T(256)S(1)} %reshape.130), kind=kCustom, calls=%fused_computation.clone | custom fusion | bytes 22528 | tf_op jit(solution)/shard_map/jit(take_along_axis)/gather | solution.py:54
  99.0 7.0 %gather_fusion.1 = f32[256,5,2]{1,2,0:T(2,128)S(1)} fusion(f32[8,5,2,2048]{1,2,3,0:T(2,128)} %copy.77, s32[256]{0:T(256)S(1)} %reshape.135), kind=kCustom, calls=%fused_computation.1.clone | custom fusion | bytes 22528 | tf_op jit(solution)/shard_map/jit(take_along_axis)/gather | solution.py:55
  106.2 0.4 fusion.15
  106.7 0.9 reshape.143
  107.6 6.8 %all-to-all-start.3 = ((f32[16,1,1280]{2,1,0:T(1,128)}), f32[16,1,1280]{2,1,0:T(1,128)S(1)}, u32[]{:S(2)}, u32[]{:S(2)}) async-start(f32[16,1,1280]{2,1,0:T(1,128)} %reshape.143), calls=%async_computation.3 | async-start | bytes 163840 | tf_op jit(solution)/shard_map/all_to_all | solution.py:31
  114.4 6.6 %all-to-all-done.3 = f32[16,1,1280]{2,1,0:T(1,128)S(1)} async-done(((f32[16,1,1280]{2,1,0:T(1,128)}), f32[16,1,1280]{2,1,0:T(1,128)S(1)}, u32[]{:S(2)}, u32[]{:S(2)}) %all-to-all-start.3) | async-done | bytes 81952 | tf_op jit(solution)/shard_map/all_to_all | solution.py:31
  120.9 0.8 reduce.7
  121.8 0.2 reshape.144
  122.1 0.6 copy.84
  (35 shorter events, 1.9 us)
Async XLA Ops:
  2.6 20.0 %all-to-all-start = ((f32[16,1,200]{2,1,0:T(1,128)}), f32[16,1,200]{2,1,0:T(1,128)S(1)}, u32[]{:S(2)}, u32[]{:S(2)}) async-start(f32[16,1,200]{2,1,0:T(1,128)} %reshape.141), calls=%async_computation | async-start | bytes 32768 | tf_op jit(solution)/shard_map/all_to_all | solution.py:14
  21.0 33.7 %copy-start = (s32[8,512]{1,0:T(8,128)S(1)}, s32[8,512]{1,0:T(8,128)}, u32[]{:S(2)}) copy-start(s32[8,512]{1,0:T(8,128)} %param.12) | copy-start | bytes 49156
  21.0 33.9 %copy-start.1 = (s32[128]{0:T(128)S(1)}, s32[128]{0:T(128)}, u32[]{:S(2)}) copy-start(s32[128]{0:T(128)} %param.13) | copy-start | bytes 1540
  22.6 27.2 %all-to-all-start.1 = ((f32[16,8,5,256]{3,1,2,0:T(8,128)}), f32[16,8,5,256]{3,1,2,0:T(8,128)S(1)}, u32[]{:S(2)}, u32[]{:S(2)}) async-start(f32[16,8,5,256]{3,1,2,0:T(8,128)} %copy.71), calls=%async_computation.1 | async-start | bytes 1310720 | tf_op jit(solution)/shard_map/all_to_all | solution.py:31
  51.1 23.1 %all-to-all-start.2 = ((f32[16,8,5,256]{3,1,2,0:T(8,128)}), f32[16,8,5,256]{3,1,2,0:T(8,128)S(1)}, u32[]{:S(2)}, u32[]{:S(2)}) async-start(f32[16,8,5,256]{3,1,2,0:T(8,128)} %broadcast_in_dim.13), calls=%async_computation.2 | async-start | bytes 1310720 | tf_op jit(solution)/shard_map/all_to_all | solution.py:14
  107.6 13.3 %all-to-all-start.3 = ((f32[16,1,1280]{2,1,0:T(1,128)}), f32[16,1,1280]{2,1,0:T(1,128)S(1)}, u32[]{:S(2)}, u32[]{:S(2)}) async-start(f32[16,1,1280]{2,1,0:T(1,128)} %reshape.143), calls=%async_computation.3 | async-start | bytes 163840 | tf_op jit(solution)/shard_map/all_to_all | solution.py:31
where the time goes:
time: 123 us
  local copies, waits for them, and re-layouts  38.1 us (31%)
  waiting for transfers between devices  36.8 us (30%)
  starting transfers between devices  27.4 us (22%)
  other arithmetic  15.1 us (12%)
  matrix products  5.09 us (4%)
    all_to_all x2, waiting for transfers between devices, from_everyone(): lax.all_to_all(jnp.broadcast_to(value[None], (size, *value.shape)), axis,...  19 us
    all_to_all x2, waiting for transfers between devices, summed_on_arrival(): lax.all_to_all(parts, axis, split_axis=0, concat_axis=0, tiled=True)  17.8 us
    another operation x2, local copies, waits for them, and re-layouts, body(): coeff = gather_directly(solved, 'evt', 2).reshape(stations, 5, 2, NS)  17.4 us
    all_to_all x2, starting transfers between devices, summed_on_arrival(): lax.all_to_all(parts, axis, split_axis=0, concat_axis=0, tiled=True)  14 us
    all_to_all x2, starting transfers between devices, from_everyone(): lax.all_to_all(jnp.broadcast_to(value[None], (size, *value.shape)), axis,...  13.5 us
    gather x3, local copies, waits for them, and re-layouts, to_depths(): second = jnp.take_along_axis(values, picks + 1, axis=3)  7.29 us
    gather x3, local copies, waits for them, and re-layouts, to_depths(): first = jnp.take_along_axis(values, picks, axis=3)  7.28 us
    add x1, other arithmetic, body(): jnp.cos(incidence)[:, :, None] * radial  4.35 us
  transfers between devices with their start and end apart: 4, of which 3 were waited for; matrix products, arithmetic and copies ran while one was open for 16% of the time, Pallas kernels for 0%

commit v1 on v0

v1 whole, which is shorter than its diff:
```python
import jax
import jax.numpy as jnp
from jax import lax
from jax.experimental import pallas as pl
from jax.experimental.pallas import tpu as pltpu
from jax.sharding import PartitionSpec as P

NS = 2048
DEPTHS = 512
BAZ_BINS = 36
TILE_DEV = 4
STA = 8
EVT = 64
ROWS = 10
PAIRS = [(k, l) for k in range(5) for l in range(k, 5)]
CHUNKS = 4
WIDTH = NS // CHUNKS


def fit_kernel(traces, baz_ref, inc_ref, counts, depth_ref, out_ref, data, lhs, acc, sems):
    copies = []
    for n in range(CHUNKS):
        cols = pl.ds(n * WIDTH, WIDTH)
        copy = pltpu.make_async_copy(
            traces.at[:, :, :, cols], data.at[:, :, :, cols], sems.at[n]
        )
        copy.start()
        copies.append(copy)

    lane = lax.broadcasted_iota(jnp.int32, (STA, 128), 1)
    row = lax.broadcasted_iota(jnp.int32, (STA, 128), 0)
    baz = jnp.concatenate([baz_ref[...], baz_ref[...]], axis=1)
    inc = jnp.concatenate([inc_ref[...], inc_ref[...]], axis=1)
    phi = (baz.astype(jnp.float32) + 0.5) * (2.0 * jnp.pi / BAZ_BINS)
    tilt = (12.0 + 2.5 * (inc.astype(jnp.float32) + 0.5)) * (jnp.pi / 180.0)
    cosine = jnp.cos(phi)
    sine = jnp.sin(phi)
    cos_inc = jnp.cos(tilt)
    sin_inc = jnp.sin(tilt)
    total = jnp.zeros((STA, 128), jnp.int32)
    for s in range(STA):
        total = jnp.where(row == s, counts[s], total)
    slot = lax.axis_index("evt") * EVT + (lane & (EVT - 1))
    live = (slot < total).astype(jnp.float32)
    harm = [
        jnp.ones_like(phi),
        cosine,
        sine,
        1.0 - 2.0 * sine * sine,
        2.0 * sine * cosine,
    ]
    weighted = [h * live for h in harm]

    normal = jnp.zeros((STA, 128), jnp.float32)
    for i, (k, l) in enumerate(PAIRS):
        entry = jnp.where(lane < EVT, weighted[k] * harm[l], 0.0)
        normal = jnp.where(lane == 64 + i, jnp.sum(entry, axis=1, keepdims=True), normal)

    quality = [sin_inc, -cos_inc * cosine, -cos_inc * sine]
    transverse = [None, sine, -cosine]
    own = [((row >> 1) == v) & ((lane >> 6) == (row & 1)) for v in range(4)]
    for comp in range(3):
        for v in range(4):
            parts = []
            for split in range(2):
                for k in range(5):
                    for base in (quality[comp], transverse[comp]):
                        if base is None:
                            parts.append(jnp.zeros((STA, 128), jnp.float32))
                            continue
                        value = weighted[k] * base
                        high = value.astype(jnp.bfloat16).astype(jnp.float32)
                        piece = high if split == 0 else value - high
                        parts.append(jnp.where(own[v], piece, 0.0))
            block = jnp.concatenate(parts, axis=0).astype(jnp.bfloat16)
            lhs[:, pl.ds((comp * 4 + v) * 128, 128)] = block

    for n in range(CHUNKS):
        copies[n].wait()
        cols = pl.ds(n * WIDTH, WIDTH)
        block = data[:, :, :, cols].reshape(3 * STA * EVT, WIDTH)
        product = jnp.dot(lhs[...], block, preferred_element_type=jnp.float32)
        acc[:, cols] = product[: ROWS * STA] + product[ROWS * STA :]

    depth = depth_ref[...]
    rolled = []
    for b in range(4):
        piece = depth[:, b * 128 : (b + 1) * 128]
        for q in range(4):
            moved = pltpu.roll(piece, q * 32, 1) if q else piece
            rolled.append((moved >> 7, moved & 127))
    group = lane >> 5
    picked = {}
    for r in range(ROWS):
        q = r % 4
        strips = [acc[pl.ds(r * STA, STA), pl.ds(b * 128, 128)] for b in range(16)]
        turned = [pltpu.roll(strip, 127, 1) for strip in strips]
        means = []
        for b in range(16):
            after = turned[b] if b == 15 else jnp.where(lane == 127, turned[b + 1], turned[b])
            means.append(0.5 * (strips[b] + after))
        for b in range(4):
            high, low = rolled[b * 4 + q]
            result = jnp.take_along_axis(means[0], low, axis=1)
            for t in range(1, 16):
                result = jnp.where(high == t, jnp.take_along_axis(means[t], low, axis=1), result)
            picked[r, b] = result
    for b in range(4):
        for jj in range(4):
            for g in range(3):
                value = None
                for p in range(4):
                    r = 4 * g + (p - jj) % 4
                    if r >= ROWS:
                        if r > ROWS:
                            continue
                        source = pltpu.roll(normal, jj * 32, 1) if jj else normal
                        where = (group == p) | (group == (p + 1) % 4)
                    else:
                        source = picked[r, b]
                        where = group == p
                    value = source if value is None else jnp.where(where, source, value)
                out_ref[b * 4 + jj, pl.ds(g * 8, 8), :] = value


def solve_kernel(parts_ref, tile_ref, out_ref):
    lane = lax.broadcasted_iota(jnp.int32, (STA, 128), 1)
    total = jnp.sum(parts_ref[...], axis=0)
    back = lax.rem(4 - lax.rem(lax.axis_index("evt"), 4), 4) * 32
    mine = [pltpu.roll(total[g * 8 : (g + 1) * 8], back, 1) for g in range(3)]
    entry = {}
    for i, (k, l) in enumerate(PAIRS):
        value = jnp.broadcast_to(mine[2][:, 64 + i : 65 + i], (STA, 128))
        entry[k, l] = value + 1.0 if k == l else value
    right = []
    for k in range(5):
        right.append(pltpu.roll(mine[k // 2], 64, 1) if k % 2 else mine[k // 2])
    inverse = []
    for k in range(5):
        inv = 1.0 / entry[k, k]
        inverse.append(inv)
        for l in range(k + 1, 5):
            factor = entry[k, l] * inv
            for m in range(l, 5):
                entry[l, m] = entry[l, m] - factor * entry[k, m]
            right[l] = right[l] - factor * right[k]
    solved = [None] * 5
    for k in reversed(range(5)):
        value = right[k]
        for l in range(k + 1, 5):
            value = value - entry[k, l] * solved[l]
        solved[k] = value * inverse[k]
    low = lane < 64
    joined = jnp.concatenate(
        [
            jnp.where(low, solved[0], pltpu.roll(solved[1], 64, 1)),
            jnp.where(low, solved[2], pltpu.roll(solved[3], 64, 1)),
            jnp.where(low, solved[4], 0.0),
        ],
        axis=1,
    )
    shift = lax.rem(128 - lax.axis_index("sta") * STA, 128)
    local = pltpu.roll(jnp.broadcast_to(tile_ref[...], (8, 128)), shift, 1)[0:1, 0:STA]
    ids = lax.broadcasted_iota(jnp.int32, (64, STA), 0)
    onehot = (jnp.broadcast_to(local, (64, STA)) == ids).astype(jnp.float32)
    sums = jnp.dot(
        onehot, joined, precision=lax.Precision.HIGHEST, preferred_element_type=jnp.float32
    )
    for i in range(16):
        out_ref[i] = sums[i * TILE_DEV : (i + 1) * TILE_DEV]


def stack_kernel(parts_ref, tile_ref, out_ref):
    sums = jnp.sum(parts_ref[...], axis=0)
    own = lax.axis_index("sta") * TILE_DEV + lax.broadcasted_iota(jnp.int32, (TILE_DEV, 128), 0)
    match = (jnp.broadcast_to(tile_ref[...], (TILE_DEV, 128)) == own).astype(jnp.float32)
    members = jnp.sum(match, axis=1, keepdims=True)
    result = sums / jnp.maximum(members, 1.0)
    for k in range(5):
        for c in range(2):
            out_ref[:, k, c, :] = result[:, k * 64 + c * 32 : k * 64 + c * 32 + 32]


def body(traces, baz_bin, inc_bin, counts, depth_index, tile_of):
    vmem = pl.BlockSpec(memory_space=pltpu.VMEM)
    partial = pl.pallas_call(
        fit_kernel,
        out_shape=jax.ShapeDtypeStruct((16, 24, 128), jnp.float32),
        in_specs=[
            pl.BlockSpec(memory_space=pl.ANY),
            vmem,
            vmem,
            pl.BlockSpec(memory_space=pltpu.SMEM),
            vmem,
        ],
        out_specs=vmem,
        scratch_shapes=[
            pltpu.VMEM((3, STA, EVT, NS), jnp.bfloat16),
            pltpu.VMEM((2 * ROWS * STA, 3 * STA * EVT), jnp.bfloat16),
            pltpu.VMEM((ROWS * STA, NS), jnp.float32),
            pltpu.SemaphoreType.DMA((CHUNKS,)),
        ],
        name="fit",
    )(traces, baz_bin, inc_bin, counts, depth_index)
    arrived = lax.all_to_all(partial, "evt", 0, 0, tiled=True)
    tiles = tile_of.reshape(1, 128)
    sums = pl.pallas_call(
        solve_kernel,
        out_shape=jax.ShapeDtypeStruct((16, TILE_DEV, 384), jnp.float32),
        in_specs=[vmem, vmem],
        out_specs=vmem,
        name="solve",
    )(arrived, tiles)
    landed = lax.all_to_all(sums, "sta", 0, 0, tiled=True)
    return pl.pallas_call(
        stack_kernel,
        out_shape=jax.ShapeDtypeStruct((TILE_DEV, 5, 2, 32), jnp.float32),
        in_specs=[vmem, vmem],
        out_specs=vmem,
        name="stack",
    )(landed, tiles)


def solution(mesh):
    return jax.shard_map(
        body,
        mesh=mesh,
        in_specs=(
            P(None, "sta", "evt", None),
            P("sta", "evt"),
            P("sta", "evt"),
            P("sta"),
            P("sta", None),
            P(),
        ),
        out_specs=P("sta", None, None, "evt"),
        check_vma=False,
    )
```

time: 123 us -> 44.7 us (0.36)
  local copies, waits for them, and re-layouts: 38.1 us -> 0 us
  waiting for transfers between devices: 36.8 us -> 0 us
  blocking collectives: 0 us -> 34.1 us
  starting transfers between devices: 27.4 us -> 0 us
  other arithmetic: 15.1 us -> 0 us
  Pallas kernels: 0 us -> 10.2 us
  matrix products: 5.09 us -> 0 us
    all_to_all x4 -> x0, waiting for transfers between devices: 36.8 us -> none  [the longest x2 19 us: from_everyone(): lax.all_to_all(jnp.broadcast_to(value[None], (size, *value.shape)), axis,...]
    all_to_all x0 -> x2, blocking collectives: none -> 34.1 us  [the longest x1 20.3 us: body(): arrived = lax.all_to_all(partial, 'evt', 0, 0, tiled=True)]
    all_to_all x4 -> x0, starting transfers between devices: 27.4 us -> none  [the longest x2 14 us: summed_on_arrival(): lax.all_to_all(parts, axis, split_axis=0, concat_axis=0, tiled=True)]
    another operation x5 -> x0, local copies, waits for them, and re-layouts: 17.5 us -> none  [the longest x2 17.4 us: body(): coeff = gather_directly(solved, 'evt', 2).reshape(stations, 5, 2, NS)]
    gather x6 -> x0, local copies, waits for them, and re-layouts: 14.6 us -> none  [the longest x3 7.29 us: to_depths(): second = jnp.take_along_axis(values, picks + 1, axis=3)]
    pallas_call x0 -> x3, Pallas kernels: none -> 10.2 us  [the longest x1 6.46 us: body(): pl.pallas_call(fit_kernel, out_shape=jax.ShapeDtypeStruct((16, 24, 128),...]
    another operation x7 -> x0, other arithmetic: 7.1 us -> none  [the longest x4 3.83 us: solve_blocks(): factor = jnp.linalg.cholesky(normal)]
    dot_general x3 -> x0, matrix products: 4.64 us -> none  [the longest x1 4.04 us: body(): rhs_part = jnp.einsum('sek,sec->skc', weighted, data, precision=highest)]
  transfers between devices with their start and end apart: 4 -> 0, of which waited for: 3 -> 0; matrix products, arithmetic and copies ran while one was open for 16% -> 0% of each run, Pallas kernels for 0% -> 0%
where the time goes in v1:
time: 44.7 us; the launch traced here: 44.3 us
  blocking collectives  34.1 us (76%)
  Pallas kernels  10.2 us (23%)
    all_to_all x1, blocking collectives, body(): arrived = lax.all_to_all(partial, 'evt', 0, 0, tiled=True)  20.3 us
    all_to_all x1, blocking collectives, body(): landed = lax.all_to_all(sums, 'sta', 0, 0, tiled=True)  13.8 us
    pallas_call x1, Pallas kernels, body(): pl.pallas_call(fit_kernel, out_shape=jax.ShapeDtypeStruct((16, 24, 128),...  6.46 us
    pallas_call x1, Pallas kernels, body(): pl.pallas_call(solve_kernel, out_shape=jax.ShapeDtypeStruct((16, TILE_DEV...  2.05 us
    pallas_call x1, Pallas kernels, body(): pl.pallas_call(stack_kernel, out_shape=jax.ShapeDtypeStruct((TILE_DEV, 5,...  1.7 us

profile of v1, /device:TPU:1, one launch (start us, length us, event | category | flops | bytes accessed | tf_op | source)
XLA Modules:
  0.0 44.3 jit_solution(3003725923263842861)
XLA Ops:
  0.0 6.5 %fit.1 = f32[16,24,128]{2,1,0:T(8,128)} custom-call(bf16[3,8,64,2048]{3,2,1,0:T(8,128)(2,1)} %traces.1, s32[8,64]{1,0:T(8,128)} %baz_ref.1, s32[8,64]{1,0:T(8,128)} %inc_ref.1, s32[8]{0:T(128)} %counts.1, s32[8,512]{1,0:T(8,128)} %depth_ref.1), custom_call_target="tpu_custom_call" | custom-call | tf_op jit(solution)/shard_map/fit/pallas_call | solution.py:186
  6.5 20.3 %all_to_all.10.parts_ref = f32[16,24,128]{2,1,0:T(8,128)} all-to-all(f32[16,24,128]{2,1,0:T(8,128)} %fit.1), channel_id=1, replica_groups=mesh['sta'=16,'evt'=16] {'evt'}, dimensions={0} | all-to-all | bytes 393216 | tf_op jit(solution)/shard_map/all_to_all | solution.py:205
  26.7 2.1 %solve.1 = f32[16,4,384]{2,1,0:T(4,128)} custom-call(f32[16,24,128]{2,1,0:T(8,128)} %all_to_all.10.parts_ref, s32[1,128]{1,0:T(1,128)} %bitcast.1), custom_call_target="tpu_custom_call" | custom-call | tf_op jit(solution)/shard_map/solve/pallas_call | solution.py:207
  28.8 13.8 %all_to_all.11.parts_ref = f32[16,4,384]{2,1,0:T(4,128)} all-to-all(f32[16,4,384]{2,1,0:T(4,128)} %solve.1), channel_id=1, replica_groups=mesh['sta'=16,'evt'=16] {'sta'}, dimensions={0} | all-to-all | bytes 196608 | tf_op jit(solution)/shard_map/all_to_all | solution.py:214
  42.6 1.7 %stack.1 = f32[4,5,2,32]{3,2,1,0:T(2,128)} custom-call(f32[16,4,384]{2,1,0:T(4,128)} %all_to_all.11.parts_ref, s32[1,128]{1,0:T(1,128)} %bitcast.2), custom_call_target="tpu_custom_call" | custom-call | tf_op jit(solution)/shard_map/stack/pallas_call | solution.py:215

commit v2 on v1

--- a/solution.py
+++ b/solution.py
@@ -17,7 +17,17 @@
 WIDTH = NS // CHUNKS
 
 
-def fit_kernel(traces, baz_ref, inc_ref, counts, depth_ref, out_ref, data, lhs, acc, sems):
+def fit_kernel(
+    traces, baz_bin, inc_bin, counts_in, depth_index, out_ref,
+    data, lhs, acc, baz_ref, inc_ref, counts, depth_ref, sems,
+):
+    small = []
+    for i, (source, target) in enumerate(
+        ((baz_bin, baz_ref), (inc_bin, inc_ref), (counts_in, counts), (depth_index, depth_ref))
+    ):
+        copy = pltpu.make_async_copy(source, target, sems.at[CHUNKS + i])
+        copy.start()
+        small.append(copy)
     copies = []
     for n in range(CHUNKS):
         cols = pl.ds(n * WIDTH, WIDTH)
@@ -27,6 +37,8 @@
         copy.start()
         copies.append(copy)
 
+    for copy in small:
+        copy.wait()
     lane = lax.broadcasted_iota(jnp.int32, (STA, 128), 1)
     row = lax.broadcasted_iota(jnp.int32, (STA, 128), 0)
     baz = jnp.concatenate([baz_ref[...], baz_ref[...]], axis=1)
@@ -186,22 +198,21 @@
     partial = pl.pallas_call(
         fit_kernel,
         out_shape=jax.ShapeDtypeStruct((16, 24, 128), jnp.float32),
-        in_specs=[
-            pl.BlockSpec(memory_space=pl.ANY),
-            vmem,
-            vmem,
-            pl.BlockSpec(memory_space=pltpu.SMEM),
-            vmem,
-        ],
+        in_specs=[pl.BlockSpec(memory_space=pltpu.HBM)] * 5,
         out_specs=vmem,
         scratch_shapes=[
             pltpu.VMEM((3, STA, EVT, NS), jnp.bfloat16),
             pltpu.VMEM((2 * ROWS * STA, 3 * STA * EVT), jnp.bfloat16),
             pltpu.VMEM((ROWS * STA, NS), jnp.float32),
-            pltpu.SemaphoreType.DMA((CHUNKS,)),
+            pltpu.VMEM((STA, EVT), jnp.int32),
+            pltpu.VMEM((STA, EVT), jnp.int32),
+            pltpu.SMEM((STA,), jnp.int32),
+            pltpu.VMEM((STA, DEPTHS), jnp.int32),
+            pltpu.SemaphoreType.DMA((CHUNKS + 4,)),
         ],
+        compiler_params=pltpu.CompilerParams(vmem_limit_bytes=16 << 20),
         name="fit",
-    )(traces, baz_bin, inc_bin, counts, depth_index)
+    )(*(pltpu.with_memory_space_constraint(x, pltpu.HBM) for x in (traces, baz_bin, inc_bin, counts, depth_index)))
     arrived = lax.all_to_all(partial, "evt", 0, 0, tiled=True)
     tiles = tile_of.reshape(1, 128)
     sums = pl.pallas_call(
@@ -209,6 +220,7 @@
         out_shape=jax.ShapeDtypeStruct((16, TILE_DEV, 384), jnp.float32),
         in_specs=[vmem, vmem],
         out_specs=vmem,
+        compiler_params=pltpu.CompilerParams(vmem_limit_bytes=4 << 20),
         name="solve",
     )(arrived, tiles)
     landed = lax.all_to_all(sums, "sta", 0, 0, tiled=True)
@@ -217,6 +229,7 @@
         out_shape=jax.ShapeDtypeStruct((TILE_DEV, 5, 2, 32), jnp.float32),
         in_specs=[vmem, vmem],
         out_specs=vmem,
+        compiler_params=pltpu.CompilerParams(vmem_limit_bytes=4 << 20),
         name="stack",
     )(landed, tiles)
 

time: 44.7 us -> 40 us (0.89)
  Pallas kernels: 10.2 us -> 6.37 us
  blocking collectives: 34.1 us -> 33.5 us
    pallas_call x1, Pallas kernels: 2.05 us -> 0.49 us  [body(): pl.pallas_call(solve_kernel, out_shape=jax.ShapeDtypeStruct((16, TILE_DEV...]
    pallas_call x1, Pallas kernels: 6.46 us -> 5.08 us  [body(): pl.pallas_call(fit_kernel, out_shape=jax.ShapeDtypeStruct((16, 24, 128),...]
    pallas_call x1, Pallas kernels: 1.7 us -> 0.81 us  [body(): pl.pallas_call(stack_kernel, out_shape=jax.ShapeDtypeStruct((TILE_DEV, 5,...]
where the time goes in v2:
time: 40 us; the launch traced here: 39.9 us
  blocking collectives  33.5 us (84%)
  Pallas kernels  6.37 us (16%)
    all_to_all x1, blocking collectives, body(): arrived = lax.all_to_all(partial, 'evt', 0, 0, tiled=True)  20 us
    all_to_all x1, blocking collectives, body(): landed = lax.all_to_all(sums, 'sta', 0, 0, tiled=True)  13.5 us
    pallas_call x1, Pallas kernels, body(): pl.pallas_call(fit_kernel, out_shape=jax.ShapeDtypeStruct((16, 24, 128),...  5.08 us
    pallas_call x1, Pallas kernels, body(): pl.pallas_call(stack_kernel, out_shape=jax.ShapeDtypeStruct((TILE_DEV, 5,...  0.81 us

profile of v2, /device:TPU:1, one launch (start us, length us, event | category | flops | bytes accessed | tf_op | source)
XLA Modules:
  0.0 39.9 jit_solution(6873253599890125767)
XLA Ops:
  0.0 0.0 copy-start
  0.0 5.1 %fit.1 = f32[16,24,128]{2,1,0:T(8,128)S(1)} custom-call(bf16[3,8,64,2048]{3,2,1,0:T(8,128)(2,1)} %traces.1, s32[8,64]{1,0:T(8,128)} %baz_bin.1, s32[8,64]{1,0:T(8,128)} %inc_bin.1, s32[8]{0:T(128)} %counts_in.1, s32[8,512]{1,0:T(8,128)} %depth_index.1), custom_call_target="tpu_custom_call" | custom-call | tf_op jit(solution)/shard_map/fit/pallas_call | solution.py:198
  5.1 20.0 %all_to_all.10.parts_ref = f32[16,24,128]{2,1,0:T(8,128)S(1)} all-to-all(f32[16,24,128]{2,1,0:T(8,128)S(1)} %fit.1), channel_id=1, replica_groups=mesh['sta'=16,'evt'=16] {'evt'}, dimensions={0} | all-to-all | bytes 393216 | tf_op jit(solution)/shard_map/all_to_all | solution.py:216
  25.0 0.0 copy-done
  25.0 0.5 %solve.1 = f32[16,4,384]{2,1,0:T(4,128)S(1)} custom-call(f32[16,24,128]{2,1,0:T(8,128)S(1)} %all_to_all.10.parts_ref, s32[1,128]{1,0:T(1,128)S(1)} %bitcast.1), custom_call_target="tpu_custom_call" | custom-call | tf_op jit(solution)/shard_map/solve/pallas_call | solution.py:218
  25.5 13.5 %all_to_all.11.parts_ref = f32[16,4,384]{2,1,0:T(4,128)S(1)} all-to-all(f32[16,4,384]{2,1,0:T(4,128)S(1)} %solve.1), channel_id=1, replica_groups=mesh['sta'=16,'evt'=16] {'sta'}, dimensions={0} | all-to-all | bytes 196608 | tf_op jit(solution)/shard_map/all_to_all | solution.py:226
  39.1 0.8 %stack.1 = f32[4,5,2,32]{3,2,1,0:T(2,128)} custom-call(f32[16,4,384]{2,1,0:T(4,128)S(1)} %all_to_all.11.parts_ref, s32[1,128]{1,0:T(1,128)S(1)} %bitcast.2), custom_call_target="tpu_custom_call" | custom-call | tf_op jit(solution)/shard_map/stack/pallas_call | solution.py:227
Async XLA Ops:
  0.0 25.0 %copy-start = (s32[128]{0:T(128)S(1)}, s32[128]{0:T(128)}, u32[]{:S(2)}) copy-start(s32[128]{0:T(128)} %param.11) | copy-start | bytes 1540

commit v3 on v2

--- a/solution.py
+++ b/solution.py
@@ -13,13 +13,14 @@
 EVT = 64
 ROWS = 10
 PAIRS = [(k, l) for k in range(5) for l in range(k, 5)]
-CHUNKS = 4
-WIDTH = NS // CHUNKS
+WIDTHS = (512,)*4
+STARTS = tuple(range(0,2048,512))
+CHUNKS = len(WIDTHS)
 
 
 def fit_kernel(
     traces, baz_bin, inc_bin, counts_in, depth_index, out_ref,
-    data, lhs, acc, baz_ref, inc_ref, counts, depth_ref, sems,
+    data, lhs, acc, mean, picked, baz_ref, inc_ref, counts, depth_ref, sems,
 ):
     small = []
     for i, (source, target) in enumerate(
@@ -30,7 +31,7 @@
         small.append(copy)
     copies = []
     for n in range(CHUNKS):
-        cols = pl.ds(n * WIDTH, WIDTH)
+        cols = pl.ds(STARTS[n], WIDTHS[n])
         copy = pltpu.make_async_copy(
             traces.at[:, :, :, cols], data.at[:, :, :, cols], sems.at[n]
         )
@@ -87,36 +88,48 @@
             block = jnp.concatenate(parts, axis=0).astype(jnp.bfloat16)
             lhs[:, pl.ds((comp * 4 + v) * 128, 128)] = block
 
+    depth = depth_ref[...]
+
+    def pick(first, last):
+        means = []
+        for r in range(ROWS):
+            rows = pl.ds(r * STA, STA)
+            strips = [acc[rows, pl.ds(t * 128, 128)] for t in range(first, min(last + 1, 16))]
+            turned = [pltpu.roll(strip, 127, 1) for strip in strips]
+            for t in range(last - first):
+                after = turned[t]
+                if t + 1 < len(turned):
+                    after = jnp.where(lane == 127, turned[t + 1], after)
+                mean[r, first + t] = 0.5 * (strips[t] + after)
+        for b in range(4):
+            piece = depth[:, b * 128 : (b + 1) * 128]
+            high, low = piece >> 7, piece & 127
+            for r in range(ROWS):
+                result = picked[r * 4 + b] if first else jnp.zeros((STA, 128), jnp.float32)
+                for t in range(first, last):
+                    result = jnp.where(
+                        high == t, jnp.take_along_axis(mean[r, t], low, axis=1), result
+                    )
+                picked[r * 4 + b] = result
+
+    done = 0
     for n in range(CHUNKS):
         copies[n].wait()
-        cols = pl.ds(n * WIDTH, WIDTH)
-        block = data[:, :, :, cols].reshape(3 * STA * EVT, WIDTH)
+        cols = pl.ds(STARTS[n], WIDTHS[n])
+        block = data[:, :, :, cols].reshape(3 * STA * EVT, WIDTHS[n])
         product = jnp.dot(lhs[...], block, preferred_element_type=jnp.float32)
         acc[:, cols] = product[: ROWS * STA] + product[ROWS * STA :]
-
-    depth = depth_ref[...]
-    rolled = []
-    for b in range(4):
-        piece = depth[:, b * 128 : (b + 1) * 128]
-        for q in range(4):
-            moved = pltpu.roll(piece, q * 32, 1) if q else piece
-            rolled.append((moved >> 7, moved & 127))
+        ready = STARTS[n] // 128 - 1
+        if ready > done:
+            pick(done, ready)
+            done = ready
+    pick(done, 16)
     group = lane >> 5
-    picked = {}
-    for r in range(ROWS):
-        q = r % 4
-        strips = [acc[pl.ds(r * STA, STA), pl.ds(b * 128, 128)] for b in range(16)]
-        turned = [pltpu.roll(strip, 127, 1) for strip in strips]
-        means = []
-        for b in range(16):
-            after = turned[b] if b == 15 else jnp.where(lane == 127, turned[b + 1], turned[b])
-            means.append(0.5 * (strips[b] + after))
-        for b in range(4):
-            high, low = rolled[b * 4 + q]
-            result = jnp.take_along_axis(means[0], low, axis=1)
-            for t in range(1, 16):
-                result = jnp.where(high == t, jnp.take_along_axis(means[t], low, axis=1), result)
-            picked[r, b] = result
+    turned = {
+        (r, b): pltpu.roll(picked[r * 4 + b], (r % 4) * 32, 1) if r % 4 else picked[r * 4 + b]
+        for r in range(ROWS)
+        for b in range(4)
+    }
     for b in range(4):
         for jj in range(4):
             for g in range(3):
@@ -129,7 +142,7 @@
                         source = pltpu.roll(normal, jj * 32, 1) if jj else normal
                         where = (group == p) | (group == (p + 1) % 4)
                     else:
-                        source = picked[r, b]
+                        source = turned[r, b]
                         where = group == p
                     value = source if value is None else jnp.where(where, source, value)
                 out_ref[b * 4 + jj, pl.ds(g * 8, 8), :] = value
@@ -204,6 +217,8 @@
             pltpu.VMEM((3, STA, EVT, NS), jnp.bfloat16),
             pltpu.VMEM((2 * ROWS * STA, 3 * STA * EVT), jnp.bfloat16),
             pltpu.VMEM((ROWS * STA, NS), jnp.float32),
+            pltpu.VMEM((ROWS, 16, STA, 128), jnp.float32),
+            pltpu.VMEM((ROWS * 4, STA, 128), jnp.float32),
             pltpu.VMEM((STA, EVT), jnp.int32),
             pltpu.VMEM((STA, EVT), jnp.int32),
             pltpu.SMEM((STA,), jnp.int32),

time: 40 us -> 38.9 us (0.972)
  Pallas kernels: 6.37 us -> 5.25 us
    pallas_call x1, Pallas kernels: 5.08 us -> 3.95 us  [body(): pl.pallas_call(fit_kernel, out_shape=jax.ShapeDtypeStruct((16, 24, 128),...]
where the time goes in v3:
time: 38.9 us; the launch traced here: 38.8 us
  blocking collectives  33.5 us (86%)
  Pallas kernels  5.25 us (13%)
    all_to_all x1, blocking collectives, body(): arrived = lax.all_to_all(partial, 'evt', 0, 0, tiled=True)  20 us
    all_to_all x1, blocking collectives, body(): landed = lax.all_to_all(sums, 'sta', 0, 0, tiled=True)  13.5 us
    pallas_call x1, Pallas kernels, body(): pl.pallas_call(fit_kernel, out_shape=jax.ShapeDtypeStruct((16, 24, 128),...  3.95 us
    pallas_call x1, Pallas kernels, body(): pl.pallas_call(stack_kernel, out_shape=jax.ShapeDtypeStruct((TILE_DEV, 5,...  0.81 us

profile of v3, /device:TPU:1, one launch (start us, length us, event | category | flops | bytes accessed | tf_op | source)
XLA Modules:
  0.0 38.8 jit_solution(3303270491544670570)
XLA Ops:
  0.0 0.0 copy-start
  0.0 4.0 %fit.1 = f32[16,24,128]{2,1,0:T(8,128)S(1)} custom-call(bf16[3,8,64,2048]{3,2,1,0:T(8,128)(2,1)} %traces.1, s32[8,64]{1,0:T(8,128)} %baz_bin.1, s32[8,64]{1,0:T(8,128)} %inc_bin.1, s32[8]{0:T(128)} %counts_in.1, s32[8,512]{1,0:T(8,128)} %depth_index.1), custom_call_target="tpu_custom_call" | custom-call | tf_op jit(solution)/shard_map/fit/pallas_call | solution.py:211
  4.0 20.0 %all_to_all.10.parts_ref = f32[16,24,128]{2,1,0:T(8,128)S(1)} all-to-all(f32[16,24,128]{2,1,0:T(8,128)S(1)} %fit.1), channel_id=1, replica_groups=mesh['sta'=16,'evt'=16] {'evt'}, dimensions={0} | all-to-all | bytes 393216 | tf_op jit(solution)/shard_map/all_to_all | solution.py:231
  23.9 0.0 copy-done
  23.9 0.5 %solve.1 = f32[16,4,384]{2,1,0:T(4,128)S(1)} custom-call(f32[16,24,128]{2,1,0:T(8,128)S(1)} %all_to_all.10.parts_ref, s32[1,128]{1,0:T(1,128)S(1)} %bitcast.1), custom_call_target="tpu_custom_call" | custom-call | tf_op jit(solution)/shard_map/solve/pallas_call | solution.py:233
  24.4 13.5 %all_to_all.11.parts_ref = f32[16,4,384]{2,1,0:T(4,128)S(1)} all-to-all(f32[16,4,384]{2,1,0:T(4,128)S(1)} %solve.1), channel_id=1, replica_groups=mesh['sta'=16,'evt'=16] {'sta'}, dimensions={0} | all-to-all | bytes 196608 | tf_op jit(solution)/shard_map/all_to_all | solution.py:241
  37.9 0.8 %stack.1 = f32[4,5,2,32]{3,2,1,0:T(2,128)} custom-call(f32[16,4,384]{2,1,0:T(4,128)S(1)} %all_to_all.11.parts_ref, s32[1,128]{1,0:T(1,128)S(1)} %bitcast.2), custom_call_target="tpu_custom_call" | custom-call | tf_op jit(solution)/shard_map/stack/pallas_call | solution.py:242
Async XLA Ops:
  0.0 23.9 %copy-start = (s32[128]{0:T(128)S(1)}, s32[128]{0:T(128)}, u32[]{:S(2)}) copy-start(s32[128]{0:T(128)} %param.11) | copy-start | bytes 1540

commit v4 on v3

--- a/solution.py
+++ b/solution.py
@@ -9,6 +9,8 @@
 DEPTHS = 512
 BAZ_BINS = 36
 TILE_DEV = 4
+EVT_ORDER = [(i + 11) % 16 for i in range(16)]
+STA_ORDER = [(i + 10) % 16 for i in range(16)]
 STA = 8
 EVT = 64
 ROWS = 10
@@ -145,7 +147,7 @@
                         source = turned[r, b]
                         where = group == p
                     value = source if value is None else jnp.where(where, source, value)
-                out_ref[b * 4 + jj, pl.ds(g * 8, 8), :] = value
+                out_ref[EVT_ORDER.index(b * 4 + jj), pl.ds(g * 8, 8), :] = value
 
 
 def solve_kernel(parts_ref, tile_ref, out_ref):
@@ -192,7 +194,7 @@
         onehot, joined, precision=lax.Precision.HIGHEST, preferred_element_type=jnp.float32
     )
     for i in range(16):
-        out_ref[i] = sums[i * TILE_DEV : (i + 1) * TILE_DEV]
+        out_ref[STA_ORDER.index(i)] = sums[i * TILE_DEV : (i + 1) * TILE_DEV]
 
 
 def stack_kernel(parts_ref, tile_ref, out_ref):
@@ -228,7 +230,7 @@
         compiler_params=pltpu.CompilerParams(vmem_limit_bytes=16 << 20),
         name="fit",
     )(*(pltpu.with_memory_space_constraint(x, pltpu.HBM) for x in (traces, baz_bin, inc_bin, counts, depth_index)))
-    arrived = lax.all_to_all(partial, "evt", 0, 0, tiled=True)
+    arrived = lax.all_to_all(partial, "evt", 0, 0, tiled=True, axis_index_groups=[EVT_ORDER])
     tiles = tile_of.reshape(1, 128)
     sums = pl.pallas_call(
         solve_kernel,
@@ -238,7 +240,7 @@
         compiler_params=pltpu.CompilerParams(vmem_limit_bytes=4 << 20),
         name="solve",
     )(arrived, tiles)
-    landed = lax.all_to_all(sums, "sta", 0, 0, tiled=True)
+    landed = lax.all_to_all(sums, "sta", 0, 0, tiled=True, axis_index_groups=[STA_ORDER])
     return pl.pallas_call(
         stack_kernel,
         out_shape=jax.ShapeDtypeStruct((TILE_DEV, 5, 2, 32), jnp.float32),

time: 38.9 us -> 32.5 us (0.84)
  blocking collectives: 33.5 us -> 27.1 us
    all_to_all x2, blocking collectives: 33.5 us -> 27.1 us  [the longest x1 16.7 us: body(): lax.all_to_all(partial, 'evt', 0, 0, tiled=True, axis_index_groups=[EVT_O...]
where the time goes in v4:
time: 32.5 us; the launch traced here: 32.3 us
  blocking collectives  27.1 us (83%)
  Pallas kernels  5.25 us (16%)
    all_to_all x1, blocking collectives, body(): lax.all_to_all(partial, 'evt', 0, 0, tiled=True, axis_index_groups=[EVT_O...  16.7 us
    all_to_all x1, blocking collectives, body(): lax.all_to_all(sums, 'sta', 0, 0, tiled=True, axis_index_groups=[STA_ORDER])  10.3 us
    pallas_call x1, Pallas kernels, body(): pl.pallas_call(fit_kernel, out_shape=jax.ShapeDtypeStruct((16, 24, 128),...  3.95 us
    pallas_call x1, Pallas kernels, body(): pl.pallas_call(stack_kernel, out_shape=jax.ShapeDtypeStruct((TILE_DEV, 5,...  0.81 us

profile of v4, /device:TPU:1, one launch (start us, length us, event | category | flops | bytes accessed | tf_op | source)
XLA Modules:
  0.0 32.3 jit_solution(14312446072178898914)
XLA Ops:
  0.0 0.0 copy-start
  0.0 4.0 %fit.1 = f32[16,24,128]{2,1,0:T(8,128)S(1)} custom-call(bf16[3,8,64,2048]{3,2,1,0:T(8,128)(2,1)} %traces.1, s32[8,64]{1,0:T(8,128)} %baz_bin.1, s32[8,64]{1,0:T(8,128)} %inc_bin.1, s32[8]{0:T(128)} %counts_in.1, s32[8,512]{1,0:T(8,128)} %depth_index.1), custom_call_target="tpu_custom_call" | custom-call | tf_op jit(solution)/shard_map/fit/pallas_call | solution.py:213
  4.0 16.7 %all_to_all.10.parts_ref = f32[16,24,128]{2,1,0:T(8,128)S(1)} all-to-all(f32[16,24,128]{2,1,0:T(8,128)S(1)} %fit.1), channel_id=1, replica_groups={{11,12,13,14,15,0,1,2,3,4,5,6,7,8,9,10},{27,28,29,30,31,16,17,18,19,20,..., dimensions={0} | all-to-all | bytes 393216 | tf_op jit(solution)/shard_map/all_to_all | solution.py:233
  20.7 0.0 copy-done
  20.7 0.5 %solve.1 = f32[16,4,384]{2,1,0:T(4,128)S(1)} custom-call(f32[16,24,128]{2,1,0:T(8,128)S(1)} %all_to_all.10.parts_ref, s32[1,128]{1,0:T(1,128)S(1)} %bitcast.1), custom_call_target="tpu_custom_call" | custom-call | tf_op jit(solution)/shard_map/solve/pallas_call | solution.py:235
  21.2 10.3 %all_to_all.11.parts_ref = f32[16,4,384]{2,1,0:T(4,128)S(1)} all-to-all(f32[16,4,384]{2,1,0:T(4,128)S(1)} %solve.1), channel_id=1, replica_groups={{160,176,192,208,224,240,0,16,32,48,64,80,96,112,128,144},{161,177,193,..., dimensions={0} | all-to-all | bytes 196608 | tf_op jit(solution)/shard_map/all_to_all | solution.py:243
  31.5 0.8 %stack.1 = f32[4,5,2,32]{3,2,1,0:T(2,128)} custom-call(f32[16,4,384]{2,1,0:T(4,128)S(1)} %all_to_all.11.parts_ref, s32[1,128]{1,0:T(1,128)S(1)} %bitcast.2), custom_call_target="tpu_custom_call" | custom-call | tf_op jit(solution)/shard_map/stack/pallas_call | solution.py:244
Async XLA Ops:
  0.0 20.7 %copy-start = (s32[128]{0:T(128)S(1)}, s32[128]{0:T(128)}, u32[]{:S(2)}) copy-start(s32[128]{0:T(128)} %param.11) | copy-start | bytes 1540

commit v5 on v4

--- a/solution.py
+++ b/solution.py
@@ -14,6 +14,7 @@
 STA = 8
 EVT = 64
 ROWS = 10
+SHARE = 21
 PAIRS = [(k, l) for k in range(5) for l in range(k, 5)]
 WIDTHS = (512,)*4
 STARTS = tuple(range(0,2048,512))
@@ -69,7 +70,10 @@
     normal = jnp.zeros((STA, 128), jnp.float32)
     for i, (k, l) in enumerate(PAIRS):
         entry = jnp.where(lane < EVT, weighted[k] * harm[l], 0.0)
-        normal = jnp.where(lane == 64 + i, jnp.sum(entry, axis=1, keepdims=True), normal)
+        normal = jnp.where(
+            lane == row * 16 + i, jnp.sum(entry, axis=1, keepdims=True), normal
+        )
+    normal = jnp.sum(normal, axis=0, keepdims=True)
 
     quality = [sin_inc, -cos_inc * cosine, -cos_inc * sine]
     transverse = [None, sine, -cosine]
@@ -127,37 +131,48 @@
             done = ready
     pick(done, 16)
     group = lane >> 5
-    turned = {
-        (r, b): pltpu.roll(picked[r * 4 + b], (r % 4) * 32, 1) if r % 4 else picked[r * 4 + b]
-        for r in range(ROWS)
-        for b in range(4)
-    }
+    turned = {}
+    for r in range(ROWS):
+        for b in range(4):
+            whole = picked[r * 4 + b]
+            turned[r, b] = pltpu.roll(whole, (r % 4) * 32, 1) if r % 4 else whole
+            if r >= 8:
+                turned[r + 2, b] = pltpu.roll(pltpu.roll(whole, 4, 0), (r % 4) * 32 + 64, 1)
     for b in range(4):
         for jj in range(4):
+            base = EVT_ORDER.index(b * 4 + jj) * SHARE
             for g in range(3):
-                value = None
-                for p in range(4):
-                    r = 4 * g + (p - jj) % 4
-                    if r >= ROWS:
-                        if r > ROWS:
-                            continue
-                        source = pltpu.roll(normal, jj * 32, 1) if jj else normal
-                        where = (group == p) | (group == (p + 1) % 4)
-                    else:
-                        source = turned[r, b]
-                        where = group == p
-                    value = source if value is None else jnp.where(where, source, value)
-                out_ref[EVT_ORDER.index(b * 4 + jj), pl.ds(g * 8, 8), :] = value
+                value = turned[4 * g + (3 - jj) % 4, b]
+                for p in range(3):
+                    value = jnp.where(group == p, turned[4 * g + (p - jj) % 4, b], value)
+                if g < 2:
+                    out_ref[pl.ds(base + g * 8, 8), :] = value
+                else:
+                    out_ref[pl.ds(base + 16, 4), :] = value[0:4]
+            out_ref[pl.ds(base + 20, 1), :] = normal
 
 
 def solve_kernel(parts_ref, tile_ref, out_ref):
     lane = lax.broadcasted_iota(jnp.int32, (STA, 128), 1)
-    total = jnp.sum(parts_ref[...], axis=0)
+    row = lax.broadcasted_iota(jnp.int32, (STA, 128), 0)
+    total = []
+    for start, size in ((0, 8), (8, 8), (16, 5)):
+        pieces = [parts_ref[pl.ds(j * SHARE + start, size), :] for j in range(16)]
+        while len(pieces) > 1:
+            pieces = [x + y for x, y in zip(pieces[::2], pieces[1::2])]
+        total.append(pieces[0])
+    normal = jnp.broadcast_to(total[2][4:5], (STA, 128))
+    normal = jnp.take_along_axis(normal, row * 16 + (lane & 15), axis=1)
     back = lax.rem(4 - lax.rem(lax.axis_index("evt"), 4), 4) * 32
-    mine = [pltpu.roll(total[g * 8 : (g + 1) * 8], back, 1) for g in range(3)]
+    folded = pltpu.roll(total[2][0:4], back, 1)
+    mine = [
+        pltpu.roll(total[0], back, 1),
+        pltpu.roll(total[1], back, 1),
+        jnp.concatenate([folded, pltpu.roll(folded, 64, 1)], axis=0),
+    ]
     entry = {}
     for i, (k, l) in enumerate(PAIRS):
-        value = jnp.broadcast_to(mine[2][:, 64 + i : 65 + i], (STA, 128))
+        value = jnp.broadcast_to(normal[:, i : i + 1], (STA, 128))
         entry[k, l] = value + 1.0 if k == l else value
     right = []
     for k in range(5):
@@ -212,7 +227,7 @@
     vmem = pl.BlockSpec(memory_space=pltpu.VMEM)
     partial = pl.pallas_call(
         fit_kernel,
-        out_shape=jax.ShapeDtypeStruct((16, 24, 128), jnp.float32),
+        out_shape=jax.ShapeDtypeStruct((16 * SHARE, 128), jnp.float32),
         in_specs=[pl.BlockSpec(memory_space=pltpu.HBM)] * 5,
         out_specs=vmem,
         scratch_shapes=[
@@ -230,7 +245,9 @@
         compiler_params=pltpu.CompilerParams(vmem_limit_bytes=16 << 20),
         name="fit",
     )(*(pltpu.with_memory_space_constraint(x, pltpu.HBM) for x in (traces, baz_bin, inc_bin, counts, depth_index)))
-    arrived = lax.all_to_all(partial, "evt", 0, 0, tiled=True, axis_index_groups=[EVT_ORDER])
+    arrived = lax.all_to_all(
+        partial.reshape(16, 1, SHARE * 128), "evt", 0, 0, tiled=True, axis_index_groups=[EVT_ORDER]
+    ).reshape(16 * SHARE, 128)
     tiles = tile_of.reshape(1, 128)
     sums = pl.pallas_call(
         solve_kernel,

time: 32.5 us -> 31.9 us (0.982)
  blocking collectives: 27.1 us -> 26.5 us
    all_to_all x1, blocking collectives: 16.7 us -> 16.1 us  [body(): lax.all_to_all(partial.reshape(16, 1, SHARE * 128), 'evt', 0, 0, tiled=Tr...]
where the time goes in v5:
time: 31.9 us; the launch traced here: 31.8 us
  blocking collectives  26.5 us (83%)
  Pallas kernels  5.26 us (16%)
    all_to_all x1, blocking collectives, body(): lax.all_to_all(partial.reshape(16, 1, SHARE * 128), 'evt', 0, 0, tiled=Tr...  16.1 us
    all_to_all x1, blocking collectives, body(): lax.all_to_all(sums, 'sta', 0, 0, tiled=True, axis_index_groups=[STA_ORDER])  10.3 us
    pallas_call x1, Pallas kernels, body(): pl.pallas_call(fit_kernel, out_shape=jax.ShapeDtypeStruct((16 * SHARE, 12...  3.98 us
    pallas_call x1, Pallas kernels, body(): pl.pallas_call(stack_kernel, out_shape=jax.ShapeDtypeStruct((TILE_DEV, 5,...  0.81 us

profile of v5, /device:TPU:1, one launch (start us, length us, event | category | flops | bytes accessed | tf_op | source)
XLA Modules:
  0.0 31.8 jit_solution(12650635800828433887)
XLA Ops:
  0.0 0.0 copy-start
  0.0 4.0 %fit.1 = f32[336,128]{1,0:T(8,128)S(1)} custom-call(bf16[3,8,64,2048]{3,2,1,0:T(8,128)(2,1)} %traces.1, s32[8,64]{1,0:T(8,128)} %baz_bin.1, s32[8,64]{1,0:T(8,128)} %inc_bin.1, s32[8]{0:T(128)} %counts_in.1, s32[8,512]{1,0:T(8,128)} %depth_index.1), custom_call_target="tpu_custom_call" | custom-call | tf_op jit(solution)/shard_map/fit/pallas_call | solution.py:228
  4.0 16.1 %all_to_all.10 = f32[16,1,2688]{2,1,0:T(1,128)S(1)} all-to-all(f32[16,1,2688]{2,1,0:T(1,128)S(1)} %bitcast.3), channel_id=1, replica_groups={{11,12,13,14,15,0,1,2,3,4,5,6,7,8,9,10},{27,28,29,30,31,16,17,18,19,20,..., dimensions={0} | all-to-all | bytes 344064 | tf_op jit(solution)/shard_map/all_to_all | solution.py:248
  20.1 0.0 copy-done
  20.1 0.5 %solve.1 = f32[16,4,384]{2,1,0:T(4,128)S(1)} custom-call(f32[336,128]{1,0:T(8,128)S(1)} %bitcast.4, s32[1,128]{1,0:T(1,128)S(1)} %bitcast.5), custom_call_target="tpu_custom_call" | custom-call | tf_op jit(solution)/shard_map/solve/pallas_call | solution.py:252
  20.6 10.3 %all_to_all.11.parts_ref = f32[16,4,384]{2,1,0:T(4,128)S(1)} all-to-all(f32[16,4,384]{2,1,0:T(4,128)S(1)} %solve.1), channel_id=1, replica_groups={{160,176,192,208,224,240,0,16,32,48,64,80,96,112,128,144},{161,177,193,..., dimensions={0} | all-to-all | bytes 196608 | tf_op jit(solution)/shard_map/all_to_all | solution.py:260
  31.0 0.8 %stack.1 = f32[4,5,2,32]{3,2,1,0:T(2,128)} custom-call(f32[16,4,384]{2,1,0:T(4,128)S(1)} %all_to_all.11.parts_ref, s32[1,128]{1,0:T(1,128)S(1)} %bitcast.6), custom_call_target="tpu_custom_call" | custom-call | tf_op jit(solution)/shard_map/stack/pallas_call | solution.py:261
Async XLA Ops:
  0.0 20.1 %copy-start = (s32[128]{0:T(128)S(1)}, s32[128]{0:T(128)}, u32[]{:S(2)}) copy-start(s32[128]{0:T(128)} %param.11) | copy-start | bytes 1540

commit v6 on v5

--- a/solution.py
+++ b/solution.py
@@ -9,7 +9,7 @@
 DEPTHS = 512
 BAZ_BINS = 36
 TILE_DEV = 4
-EVT_ORDER = [(i + 11) % 16 for i in range(16)]
+EVT_ORDER = [11, 0, 1, 2, 3, 14, 15, 4, 5, 12, 13, 6, 7, 8, 9, 10]
 STA_ORDER = [(i + 10) % 16 for i in range(16)]
 STA = 8
 EVT = 64
@@ -217,10 +217,10 @@
     own = lax.axis_index("sta") * TILE_DEV + lax.broadcasted_iota(jnp.int32, (TILE_DEV, 128), 0)
     match = (jnp.broadcast_to(tile_ref[...], (TILE_DEV, 128)) == own).astype(jnp.float32)
     members = jnp.sum(match, axis=1, keepdims=True)
-    result = sums / jnp.maximum(members, 1.0)
+    scale = 1.0 / jnp.maximum(members, 1.0)
     for k in range(5):
         for c in range(2):
-            out_ref[:, k, c, :] = result[:, k * 64 + c * 32 : k * 64 + c * 32 + 32]
+            out_ref[:, k, c, :] = sums[:, k * 64 + c * 32 : k * 64 + c * 32 + 32] * scale
 
 
 def body(traces, baz_bin, inc_bin, counts, depth_index, tile_of):

time: 31.9 us -> 31.9 us (level)
  no operation moved by 1% of the time
where the time goes in v6:
time: 31.9 us; the launch traced here: 31.8 us
  blocking collectives  26.5 us (83%)
  Pallas kernels  5.26 us (16%)
    all_to_all x1, blocking collectives, body(): lax.all_to_all(partial.reshape(16, 1, SHARE * 128), 'evt', 0, 0, tiled=Tr...  15.9 us
    all_to_all x1, blocking collectives, body(): lax.all_to_all(sums, 'sta', 0, 0, tiled=True, axis_index_groups=[STA_ORDER])  10.6 us
    pallas_call x1, Pallas kernels, body(): pl.pallas_call(fit_kernel, out_shape=jax.ShapeDtypeStruct((16 * SHARE, 12...  3.98 us
    pallas_call x1, Pallas kernels, body(): pl.pallas_call(stack_kernel, out_shape=jax.ShapeDtypeStruct((TILE_DEV, 5,...  0.81 us

profile of v6, /device:TPU:1, one launch (start us, length us, event | category | flops | bytes accessed | tf_op | source)
XLA Modules:
  0.0 31.8 jit_solution(690214197553736588)
XLA Ops:
  0.0 0.0 copy-start
  0.0 4.0 %fit.1 = f32[336,128]{1,0:T(8,128)S(1)} custom-call(bf16[3,8,64,2048]{3,2,1,0:T(8,128)(2,1)} %traces.1, s32[8,64]{1,0:T(8,128)} %baz_bin.1, s32[8,64]{1,0:T(8,128)} %inc_bin.1, s32[8]{0:T(128)} %counts_in.1, s32[8,512]{1,0:T(8,128)} %depth_index.1), custom_call_target="tpu_custom_call" | custom-call | tf_op jit(solution)/shard_map/fit/pallas_call | solution.py:228
  4.0 15.9 %all_to_all.10 = f32[16,1,2688]{2,1,0:T(1,128)S(1)} all-to-all(f32[16,1,2688]{2,1,0:T(1,128)S(1)} %bitcast.3), channel_id=1, replica_groups={{11,0,1,2,3,14,15,4,5,12,13,6,7,8,9,10},{27,16,17,18,19,30,31,20,21,28,..., dimensions={0} | all-to-all | bytes 344064 | tf_op jit(solution)/shard_map/all_to_all | solution.py:248
  19.9 0.0 copy-done
  19.9 0.5 %solve.1 = f32[16,4,384]{2,1,0:T(4,128)S(1)} custom-call(f32[336,128]{1,0:T(8,128)S(1)} %bitcast.4, s32[1,128]{1,0:T(1,128)S(1)} %bitcast.5), custom_call_target="tpu_custom_call" | custom-call | tf_op jit(solution)/shard_map/solve/pallas_call | solution.py:252
  20.4 10.6 %all_to_all.11.parts_ref = f32[16,4,384]{2,1,0:T(4,128)S(1)} all-to-all(f32[16,4,384]{2,1,0:T(4,128)S(1)} %solve.1), channel_id=1, replica_groups={{160,176,192,208,224,240,0,16,32,48,64,80,96,112,128,144},{161,177,193,..., dimensions={0} | all-to-all | bytes 196608 | tf_op jit(solution)/shard_map/all_to_all | solution.py:260
  31.0 0.8 %stack.1 = f32[4,5,2,32]{3,2,1,0:T(2,128)} custom-call(f32[16,4,384]{2,1,0:T(4,128)S(1)} %all_to_all.11.parts_ref, s32[1,128]{1,0:T(1,128)S(1)} %bitcast.6), custom_call_target="tpu_custom_call" | custom-call | tf_op jit(solution)/shard_map/stack/pallas_call | solution.py:261
Async XLA Ops:
  0.0 19.9 %copy-start = (s32[128]{0:T(128)S(1)}, s32[128]{0:T(128)}, u32[]{:S(2)}) copy-start(s32[128]{0:T(128)} %param.11) | copy-start | bytes 1540
